TPU v7x, 128 devices: a whole 4x4x4 slice. The times are simulated.
128 devices in a mesh: ctx: 64 (over y_lo, x, z, core), head: 2 (over y_hi).
Axes of the slice: x: 4, y: 4 (y_hi: 2, y_lo: 2; y = y_hi * 2 + y_lo), z: 4, core: 2. Of those that a mesh axis runs over, the one named last changes fastest.
Arguments:
- queries: bfloat16 [16384, 32, 128], P('ctx', 'head'), may hold values from -300 to 300
- key_rows: bfloat16 [16384, 4, 128], P('ctx', 'head'), may hold values from -6 to 6
- value_vectors: bfloat16 [16384, 4, 128], P('ctx', 'head'), may hold values from -6 to 6
- doc_ids: int32 [16384], replicated, may hold values from 0 to 2, never falling along the last dimension, each value on 1 to 7936 neighbouring positions
Outputs:
- attended: bfloat16 [16384, 32, 128], P(('ctx', 'head'))
Inputs may be any that keep to these rules, and one draw needn't show every extreme that they name: `doc_ids`: ids never fall along the pack and each prompt holds at most 7936 tokens.
All inputs are finite; a program needn't handle non-finite values.
Results may differ from a plain program's by a relative error of at most 0.008.
Values may be sent and summed in bfloat16 or wider, within the bound.
A program may use at most 64 MiB of HBM per device.

v0:
```python
import jax
import jax.numpy as jnp
from jax import lax
from jax.sharding import PartitionSpec as P


def passed_along(block, axis, distance):
    devices = range(lax.axis_size(axis))
    route = [(i - distance, i) for i in devices if i - distance in devices]
    return lax.ppermute(block, axis, route)


def body(queries, key_rows, value_vectors, doc_ids):
    tok_len, heads_here, head_dim = queries.shape
    kv_heads = key_rows.shape[1]
    head_group = heads_here // kv_heads
    inv_root = head_dim ** (-0.5)
    cycle_size = lax.axis_size("ctx")
    reach_blocks = cycle_size // 2 - 1
    ctx_index = lax.axis_index("ctx")
    query_offset = ctx_index * tok_len
    own_doc = lax.dynamic_slice_in_dim(doc_ids, query_offset, tok_len, 0)
    own_pos = query_offset + jnp.arange(tok_len, dtype=jnp.int32)
    q_grouped = queries.reshape(tok_len, kv_heads, head_group, head_dim).transpose(1, 2, 0, 3)

    def attend(state, q_heads, query_doc, query_pos, key_block, value_block, key_start):
        key_len = key_block.shape[0]
        clamped = jnp.maximum(key_start, 0)
        key_doc = lax.dynamic_slice_in_dim(doc_ids, clamped, key_len, 0)
        key_pos = key_start + jnp.arange(key_len, dtype=jnp.int32)
        visible = (
            (query_doc[:, None] == key_doc[None, :])
            & (key_pos[None, :] <= query_pos[:, None])
            & (key_pos[None, :] >= 0)
        )
        key_major = key_block.transpose(1, 0, 2)
        value_major = value_block.transpose(1, 0, 2)

        def per_group(operand):
            q_group, k_group, v_group, run_max, run_sum, run_out = operand
            scores = (
                jnp.einsum("rtd,ud->rtu", q_group, k_group, preferred_element_type=jnp.float32)
                * inv_root
            )
            masked = jnp.where(visible[None], scores, -1e30)
            new_max = jnp.maximum(run_max, jnp.max(masked, axis=-1))
            weights = jnp.where(visible[None], jnp.exp(scores - new_max[..., None]), 0.0)
            rescale = jnp.exp(run_max - new_max)
            new_sum = run_sum * rescale + jnp.sum(weights, axis=-1)
            product = jnp.einsum(
                "rtu,ud->rtd",
                weights.astype(jnp.bfloat16),
                v_group,
                preferred_element_type=jnp.float32,
            )
            new_out = run_out * rescale[..., None] + product
            return (new_max, new_sum, new_out)

        return lax.map(per_group, (q_heads, key_major, value_major) + tuple(tuple(state)))

    state = attend(
        (
            jnp.full((kv_heads, head_group, tok_len), -1e30, jnp.float32),
            jnp.zeros((kv_heads, head_group, tok_len), jnp.float32),
            jnp.zeros((kv_heads, head_group, tok_len, head_dim), jnp.float32),
        ),
        q_grouped,
        own_doc,
        own_pos,
        key_rows,
        value_vectors,
        query_offset,
    )
    window_keys, window_values = (key_rows, value_vectors)
    covered = 1
    while covered < reach_blocks + 1:
        count = min(covered, reach_blocks + 1 - covered)
        arrived = passed_along((window_keys, window_values), "ctx", covered)
        window_keys = jnp.concatenate([arrived[0], window_keys], axis=0)
        window_values = jnp.concatenate([arrived[1], window_values], axis=0)
        covered = covered + count

    def window_turn(shard_num, carry):
        begin = (shard_num * tok_len).astype(jnp.int32)
        key_piece = lax.dynamic_slice_in_dim(window_keys, begin, tok_len, 0)
        value_piece = lax.dynamic_slice_in_dim(window_values, begin, tok_len, 0)
        return attend(
            carry,
            q_grouped,
            own_doc,
            own_pos,
            key_piece,
            value_piece,
            query_offset - (reach_blocks - shard_num) * tok_len,
        )

    state = lax.fori_loop(0, reach_blocks, window_turn, tuple(state))
    finished = (state[2] / state[1][..., None]).astype(jnp.bfloat16)
    merged = finished.transpose(2, 0, 1, 3).reshape(tok_len, heads_here, head_dim)
    return lax.all_to_all(merged, "head", split_axis=0, concat_axis=1, tiled=True)


def solution(mesh):
    placed = (P("ctx", "head", None), P("ctx", "head", None), P("ctx", "head", None), P())
    return jax.shard_map(
        body, mesh=mesh, in_specs=placed, out_specs=P(("ctx", "head"), None, None), check_vma=False
    )
```

profile of v0, /device:TPU:8, one launch (start us, length us, event | category | flops | bytes accessed | tf_op | source)
XLA Modules:
  0.0 417.5 jit_solution(9664904744055996789)
XLA Ops:
  0.9 1.9 collective-permute-start.5
  2.9 8.6 %collective-permute-done.5 = bf16[256,2,128]{2,0,1:T(8,128)(2,1)S(1)} collective-permute-done((bf16[256,2,128]{2,0,1:T(8,128)(2,1)S(1)}, bf16[256,2,128]{2,0,1:T(8,128)(2,1)S(1)}, u32[]{:S(2)}, u32[]{:S(2)}) %collective-permute-start.5) | collective-permute-done | bytes 131104 | tf_op jit(solution)/shard_map/ppermute | solution.py:10
  11.5 1.9 collective-permute-start.6
  13.4 10.6 %collective-permute-done.6 = bf16[512,2,128]{2,0,1:T(8,128)(2,1)S(1)} collective-permute-done((bf16[512,2,128]{2,0,1:T(8,128)(2,1)S(1)}, bf16[512,2,128]{2,0,1:T(8,128)(2,1)S(1)}, u32[]{:S(2)}, u32[]{:S(2)}) %collective-permute-start.6) | collective-permute-done | bytes 262176 | tf_op jit(solution)/shard_map/ppermute | solution.py:10
  24.0 1.9 collective-permute-start.7
  26.8 1.9 collective-permute-start
  28.8 10.0 %collective-permute-done = bf16[256,2,128]{2,0,1:T(8,128)(2,1)S(1)} collective-permute-done((bf16[256,2,128]{2,0,1:T(8,128)(2,1)S(1)}, bf16[256,2,128]{2,0,1:T(8,128)(2,1)S(1)}, u32[]{:S(2)}, u32[]{:S(2)}) %collective-permute-start) | collective-permute-done | bytes 131104 | tf_op jit(solution)/shard_map/ppermute | solution.py:10
  43.5 10.6 %collective-permute-done.1 = bf16[512,2,128]{2,0,1:T(8,128)(2,1)S(1)} collective-permute-done((bf16[512,2,128]{2,0,1:T(8,128)(2,1)S(1)}, bf16[512,2,128]{2,0,1:T(8,128)(2,1)S(1)}, u32[]{:S(2)}, u32[]{:S(2)}) %collective-permute-start.1) | collective-permute-done | bytes 262176 | tf_op jit(solution)/shard_map/ppermute | solution.py:10
  56.1 21.6 %collective-permute-done.2 = bf16[1024,2,128]{2,0,1:T(8,128)(2,1)S(1)} collective-permute-done((bf16[1024,2,128]{2,0,1:T(8,128)(2,1)S(1)}, bf16[1024,2,128]{2,0,1:T(8,128)(2,1)S(1)}, u32[]{:S(2)}, u32[]{:S(2)}) %collective-permute-start.2) | collective-permute-done | bytes 524320 | tf_op jit(solution)/shard_map/ppermute | solution.py:10
  77.8 2.1 collective-permute-start.3
  83.9 4.1 collective-permute-start.9
  88.0 82.1 %collective-permute-done.3 = bf16[2048,2,128]{2,0,1:T(8,128)(2,1)S(1)} collective-permute-done((bf16[2048,2,128]{2,0,1:T(8,128)(2,1)S(1)}, bf16[2048,2,128]{2,0,1:T(8,128)(2,1)S(1)}, u32[]{:S(2)}, u32[]{:S(2)}) %collective-permute-start.3) | collective-permute-done | bytes 1048608 | tf_op jit(solution)/shard_map/ppermute | solution.py:10
  183.3 21.5 %collective-permute-done.4 = bf16[4096,2,128]{2,0,1:T(8,128)(2,1)} collective-permute-done((bf16[4096,2,128]{2,0,1:T(8,128)(2,1)}, bf16[4096,2,128]{2,0,1:T(8,128)(2,1)}, u32[]{:S(2)}, u32[]{:S(2)}) %collective-permute-start.4) | collective-permute-done | bytes 2097184 | tf_op jit(solution)/shard_map/ppermute | solution.py:10
  204.7 3.3 constant_dynamic-update-slice_fusion.10
  212.2 3.9 while.66
  216.1 184.6 %while.68 = (s32[]{:T(128)}, f32[2,8,256]{2,1,0:T(8,128)S(1)}, f32[2,8,256]{2,1,0:T(8,128)S(1)}, f32[2,8,256,128]{3,2,1,0:T(8,128)S(1)}, bf16[8192,2,128]{2,0,1:...) while((s32[]{:T(128)}, f32[2,8,256]{2,1,0:T(8,128)S(1)}, ...), condition=%wide.region_9.10_spmd.clone.clone, body=%wide.region_4.9_spmd.clone.clone.sunk | while | flops 274998272 | bytes 12061696 | solution.py:97
  217.9 4.1 while.69
  223.9 4.1 while.69
  229.8 4.1 while.69
  235.8 4.1 while.69
  241.7 4.1 while.69
  247.7 4.1 while.69
  253.6 4.1 while.69
  259.6 4.1 while.69
  265.5 4.1 while.69
  271.5 4.1 while.69
  277.4 4.1 while.69
  283.4 4.1 while.69
  289.3 4.1 while.69
  295.3 4.1 while.69
  301.3 4.1 while.69
  307.2 4.1 while.69
  313.2 4.1 while.69
  319.1 4.1 while.69
  325.1 4.1 while.69
  331.0 4.1 while.69
  337.0 4.1 while.69
  342.9 4.1 while.69
  348.9 4.1 while.69
  354.8 4.1 while.69
  360.8 4.1 while.69
  366.7 4.1 while.69
  372.7 4.1 while.69
  378.7 4.1 while.69
  384.6 4.1 while.69
  390.6 4.1 while.69
  396.5 4.1 while.69
  402.1 14.3 %all_to_all.18 = bf16[256,16,128]{2,1,0:T(8,128)(2,1)S(1)} all-to-all(bf16[256,16,128]{2,1,0:T(8,128)(2,1)S(1)} %bitcast.122), channel_id=1, replica_groups=mesh['ctx'=64,'head'=2] {'head'}, dimensions={0} | all-to-all | bytes 2097152 | tf_op jit(solution)/shard_map/all_to_all | solution.py:100
  (660 shorter events, 215.5 us)
Async XLA Ops:
  0.9 10.5 %collective-permute-start.5 = (bf16[256,2,128]{2,0,1:T(8,128)(2,1)S(1)}, bf16[256,2,128]{2,0,1:T(8,128)(2,1)S(1)}, u32[]{:S(2)}, u32[]{:S(2)}) collective-permute-start(bf16[256,2,128]{2,0,1:T(8,128)(2,1)S(1)} %copy.44), channel_id=1, source_target_pairs={{0,2},{2,4},{4,6},{6,8},{8,10},{10,12},{12,14},{14,16},{16,18},{18... | collective-permute-start | bytes 393224 | tf_op jit(solution)/shard_map/ppermute | solution.py:10
  11.5 12.5 %collective-permute-start.6 = (bf16[512,2,128]{2,0,1:T(8,128)(2,1)S(1)}, bf16[512,2,128]{2,0,1:T(8,128)(2,1)S(1)}, u32[]{:S(2)}, u32[]{:S(2)}) collective-permute-start(bf16[512,2,128]{2,0,1:T(8,128)(2,1)S(1)} %pad_maximum_fusion.5), channel_id=1, source_target_pairs={{0,4},{2,6},{4,8},{6,10},{8,12},{10,14},{12,16},{14,18},{16,20},{1... | collective-permute-start | bytes 786440 | tf_op jit(solution)/shard_map/ppermute | solution.py:10
  24.0 17.6 %collective-permute-start.7 = (bf16[1024,2,128]{2,0,1:T(8,128)(2,1)S(1)}, bf16[1024,2,128]{2,0,1:T(8,128)(2,1)S(1)}, u32[]{:S(2)}, u32[]{:S(2)}) collective-permute-start(bf16[1024,2,128]{2,0,1:T(8,128)(2,1)S(1)} %pad_maximum_fusion.3), channel_id=1, source_target_pairs={{0,8},{2,10},{4,12},{6,14},{8,16},{10,18},{12,20},{14,22},{16,24},... | collective-permute-start | bytes 1572872 | tf_op jit(solution)/shard_map/ppermute | solution.py:10
  26.8 12.0 %collective-permute-start = (bf16[256,2,128]{2,0,1:T(8,128)(2,1)S(1)}, bf16[256,2,128]{2,0,1:T(8,128)(2,1)S(1)}, u32[]{:S(2)}, u32[]{:S(2)}) collective-permute-start(bf16[256,2,128]{2,0,1:T(8,128)(2,1)S(1)} %copy.43), channel_id=1, source_target_pairs={{0,2},{2,4},{4,6},{6,8},{8,10},{10,12},{12,14},{14,16},{16,18},{18... | collective-permute-start | bytes 393224 | tf_op jit(solution)/shard_map/ppermute | solution.py:10
  38.8 133.9 %copy-start.10 = (bf16[256,2,128]{2,0,1:T(8,128)(2,1)}, bf16[256,2,128]{2,0,1:T(8,128)(2,1)S(1)}, u32[]{:S(2)}) copy-start(bf16[256,2,128]{2,0,1:T(8,128)(2,1)S(1)} %collective-permute-done) | copy-start | bytes 393220
  38.8 15.3 %collective-permute-start.1 = (bf16[512,2,128]{2,0,1:T(8,128)(2,1)S(1)}, bf16[512,2,128]{2,0,1:T(8,128)(2,1)S(1)}, u32[]{:S(2)}, u32[]{:S(2)}) collective-permute-start(bf16[512,2,128]{2,0,1:T(8,128)(2,1)S(1)} %pad_maximum_fusion.4), channel_id=1, source_target_pairs={{0,4},{2,6},{4,8},{6,10},{8,12},{10,14},{12,16},{14,18},{16,20},{1... | collective-permute-start | bytes 786440 | tf_op jit(solution)/shard_map/ppermute | solution.py:10
  41.5 39.4 %copy-start = (bf16[1024,2,128]{2,0,1:T(8,128)(2,1)}, bf16[1024,2,128]{2,0,1:T(8,128)(2,1)S(1)}, u32[]{:S(2)}) copy-start(bf16[1024,2,128]{2,0,1:T(8,128)(2,1)S(1)} %collective-permute-done.7) | copy-start | bytes 1572868
  41.6 38.2 %collective-permute-start.8 = (bf16[2048,2,128]{2,0,1:T(8,128)(2,1)S(1)}, bf16[2048,2,128]{2,0,1:T(8,128)(2,1)S(1)}, u32[]{:S(2)}, u32[]{:S(2)}) collective-permute-start(bf16[2048,2,128]{2,0,1:T(8,128)(2,1)S(1)} %pad_maximum_fusion.1), channel_id=1, source_target_pairs={{0,16},{2,18},{4,20},{6,22},{8,24},{10,26},{12,28},{14,30},{16,32}... | collective-permute-start | bytes 3145736 | tf_op jit(solution)/shard_map/ppermute | solution.py:10
  54.1 117.9 %copy-start.8 = (bf16[512,2,128]{2,0,1:T(8,128)(2,1)}, bf16[512,2,128]{2,0,1:T(8,128)(2,1)S(1)}, u32[]{:S(2)}) copy-start(bf16[512,2,128]{2,0,1:T(8,128)(2,1)S(1)} %collective-permute-done.1) | copy-start | bytes 786436
  54.2 23.5 %collective-permute-start.2 = (bf16[1024,2,128]{2,0,1:T(8,128)(2,1)S(1)}, bf16[1024,2,128]{2,0,1:T(8,128)(2,1)S(1)}, u32[]{:S(2)}, u32[]{:S(2)}) collective-permute-start(bf16[1024,2,128]{2,0,1:T(8,128)(2,1)S(1)} %pad_maximum_fusion.2), channel_id=1, source_target_pairs={{0,8},{2,10},{4,12},{6,14},{8,16},{10,18},{12,20},{14,22},{16,24},... | collective-permute-start | bytes 1572872 | tf_op jit(solution)/shard_map/ppermute | solution.py:10
  77.7 93.5 %copy-start.2 = (bf16[1024,2,128]{2,0,1:T(8,128)(2,1)}, bf16[1024,2,128]{2,0,1:T(8,128)(2,1)S(1)}, u32[]{:S(2)}) copy-start(bf16[1024,2,128]{2,0,1:T(8,128)(2,1)S(1)} %collective-permute-done.2) | copy-start | bytes 1572868
  77.8 5.5 %copy-start.14 = (bf16[256,2,128]{2,1,0:T(2,128)(2,1)S(1)}, bf16[256,2,128]{2,1,0:T(2,128)(2,1)}, u32[]{:S(2)}) copy-start(bf16[256,2,128]{2,1,0:T(2,128)(2,1)} %param.12) | copy-start | bytes 393220
  77.8 92.3 %collective-permute-start.3 = (bf16[2048,2,128]{2,0,1:T(8,128)(2,1)S(1)}, bf16[2048,2,128]{2,0,1:T(8,128)(2,1)S(1)}, u32[]{:S(2)}, u32[]{:S(2)}) collective-permute-start(bf16[2048,2,128]{2,0,1:T(8,128)(2,1)S(1)} %pad_maximum_fusion), channel_id=1, source_target_pairs={{0,16},{2,18},{4,20},{6,22},{8,24},{10,26},{12,28},{14,30},{16,32}... | collective-permute-start | bytes 3145736 | tf_op jit(solution)/shard_map/ppermute | solution.py:10
  79.8 4.0 copy-start.6
  83.2 90.2 %copy-start.16 = (bf16[256,2,128]{2,1,0:T(2,128)(2,1)S(1)}, bf16[256,2,128]{2,1,0:T(2,128)(2,1)}, u32[]{:S(2)}) copy-start(bf16[256,2,128]{2,1,0:T(2,128)(2,1)} %param.11) | copy-start | bytes 393220
  83.9 96.3 %collective-permute-start.9 = (bf16[4096,2,128]{2,0,1:T(8,128)(2,1)}, bf16[4096,2,128]{2,0,1:T(8,128)(2,1)}, u32[]{:S(2)}, u32[]{:S(2)}) collective-permute-start(bf16[4096,2,128]{2,0,1:T(8,128)(2,1)} %constant_dynamic-update-slice_fusion.11), channel_id=1, source_target_pairs={{0,32},{2,34},{4,36},{6,38},{8,40},{10,42},{12,44},{14,46},{16,48}... | collective-permute-start | bytes 6291464 | tf_op jit(solution)/shard_map/ppermute | solution.py:10
  170.1 4.0 copy-start.4
  174.1 30.6 %collective-permute-start.4 = (bf16[4096,2,128]{2,0,1:T(8,128)(2,1)}, bf16[4096,2,128]{2,0,1:T(8,128)(2,1)}, u32[]{:S(2)}, u32[]{:S(2)}) collective-permute-start(bf16[4096,2,128]{2,0,1:T(8,128)(2,1)} %constant_dynamic-update-slice_fusion), channel_id=1, source_target_pairs={{0,32},{2,34},{4,36},{6,38},{8,40},{10,42},{12,44},{14,46},{16,48}... | collective-permute-start | bytes 6291464 | tf_op jit(solution)/shard_map/ppermute | solution.py:10
  180.1 1.9 copy-start.7
  182.0 1.0 copy-start.1
  182.0 1.2 copy-start.15
  183.3 24.8 %copy-start.13 = (bf16[8192,2,128]{2,0,1:T(8,128)(2,1)}, bf16[8192,2,128]{2,0,1:T(8,128)(2,1)S(1)}, u32[]{:S(2)}) copy-start(bf16[8192,2,128]{2,0,1:T(8,128)(2,1)S(1)} %get-tuple-element.900) | copy-start | bytes 12582916
  183.3 24.7 %copy-start.5 = (bf16[2048,2,128]{2,0,1:T(8,128)(2,1)S(1)}, bf16[2048,2,128]{2,0,1:T(8,128)(2,1)}, u32[]{:S(2)}) copy-start(bf16[2048,2,128]{2,0,1:T(8,128)(2,1)} %copy-done.4) | copy-start | bytes 3145732
  208.0 1.2 copy-start.3
  208.0 2.0 copy-start.9
  208.0 2.7 copy-start.11
  208.0 3.4 copy-start.17
  208.0 4.1 copy-start.12
  208.0 4.1 copy-start.18
  208.1 4.1 copy-start.19
  208.1 4.1 copy-start.20
  208.1 4.1 copy-start.21
where the time goes:
time: 420 us; the launch traced here: 417 us
  waiting for transfers between devices  166 us (40%)
  local copies, waits for them, and re-layouts  85 us (20%)
  matrix products  81.4 us (19%)
  other arithmetic  43.9 us (10%)
  starting transfers between devices  21.5 us (5%)
  blocking collectives  14.3 us (3%)
  loops' own time  5.33 us (1%)
    ppermute x10, waiting for transfers between devices, passed_along(): return lax.ppermute(block, axis, route)  166 us
    dot_general x64, matrix products, per_group(): jnp.einsum('rtu,ud->rtd', weights.astype(jnp.bfloat16), v_group, preferre...  51.3 us
    transpose x31, local copies, waits for them, and re-layouts, attend(): value_major = value_block.transpose(1, 0, 2)  30.9 us
    dot_general x64, matrix products, per_group(): jnp.einsum('rtd,ud->rtu', q_group, k_group, preferred_element_type=jnp.fl...  30.1 us
    reduce_sum x64, other arithmetic, per_group(): new_sum = run_sum * rescale + jnp.sum(weights, axis=-1)  28.5 us
    dynamic_slice x31, local copies, waits for them, and re-layouts, attend(): key_doc = lax.dynamic_slice_in_dim(doc_ids, clamped, key_len, 0)  24.1 us
    ppermute x10, starting transfers between devices, passed_along(): return lax.ppermute(block, axis, route)  21.5 us
    unnamed x65, local copies, waits for them, and re-layouts  19.7 us
  transfers between devices with their start and end apart: 10, of which 8 were waited for; matrix products, arithmetic and copies ran while one was open for 4% of the time, Pallas kernels for 0%

commit v1 on v0

v1 whole, which is shorter than its diff:
```python
import functools

import jax
import jax.numpy as jnp
from jax import lax
from jax.experimental import pallas as pl
from jax.experimental.pallas import tpu as pltpu
from jax.sharding import PartitionSpec as P

F32, BF16 = jnp.float32, jnp.bfloat16
MESH = pl.DeviceIdType.MESH
LOG2E = 1.4426950408889634
FAR = -1e30
T = 512
U = 2048
KB = 256
OWN0 = 72
UNITS = 73
NEAR = ((0, 3), (0, 1), (3, 0), (1, 0))
SECOND = ((0, 0), (2, 0), (0, 2), (1, 1))
THIRD = ((1, 3), (3, 1), (3, 3), (2, 1))
LAST = ((2, 3), (1, 2), (3, 2), (2, 2))
SLABS = ((0, NEAR), (1, NEAR), (0, SECOND), (0, THIRD), (0, LAST), (1, SECOND), (1, THIRD), (1, LAST))


def kernel(scale, q_ref, kv_ref, doc_ref, out_ref, buf, aug, qaug, s_ref, acc, mm, ll, obuf, sbuf,
           lsem, ssem, rsem, osend, orecv, fsem):
    i = lax.axis_index("ctx")
    h = lax.axis_index("head")
    k = lax.rem(i, 2)
    z = lax.rem(i // 2, 4)
    x = lax.rem(i // 8, 4)
    y = i // 32
    o = 1 - k
    up = lambda a: lax.rem(a + 1, 4)
    dn = lambda a: lax.rem(a + 3, 4)
    op = lambda a: lax.rem(a + 2, 4)

    def dev(yy, xx, zz, kk, hh=None):
        return {"ctx": ((yy * 4 + xx) * 4 + zz) * 2 + kk, "head": h if hh is None else hh}

    A = lambda zz, xx, kk: (zz * 4 + xx) * 2 + kk
    B = lambda xx, zz, kk: 32 + (xx * 4 + zz) * 2 + kk
    R = lambda zz, kk: 64 + zz * 2 + kk
    right_x, left_x = dev(y, up(x), z, k), dev(y, dn(x), z, k)
    right_z, left_z = dev(y, x, up(z), k), dev(y, x, dn(z), k)
    across, other = dev(1 - y, x, z, k), dev(y, x, z, o)
    mate = dev(y, x, z, k, 1 - h)

    sends = {}
    ending = [False]

    def copy(n, src, dst, to):
        return pltpu.make_async_remote_copy(
            src_ref=buf.at[src], dst_ref=buf.at[dst], send_sem=ssem.at[n], recv_sem=rsem.at[dst],
            device_id=to, device_id_type=MESH)

    def when(cond, f):
        if cond is None:
            f()
        else:
            pl.when(cond)(f)

    def send(name, src, dst, to, cond=None):
        n = sends.setdefault(name, len(sends))

        def go():
            c = copy(n, src, dst, to)
            c.wait_send() if ending[0] else c.start()

        when(cond, go)

    def arrived(u, cond=None):
        if not ending[0]:
            when(cond, lambda: copy(0, u, u, other).wait_recv())

    own = jnp.int32(OWN0)
    a_own, b_own = A(z, x, k), B(x, z, k)
    local = [(0, own, None), (1, b_own, None), (0, a_own, y == 0)] + [(1, R(n, k), y == 0) for n in range(4)]

    def local_copy(n):
        g, u, _ = local[n]
        return pltpu.make_async_copy(kv_ref.at[g], buf.at[u], lsem.at[n])

    for n in range(len(local)):
        when(local[n][2], lambda n=n: local_copy(n).start())
    barrier = pltpu.get_barrier_semaphore()
    for to in (right_x, left_x, right_z, left_z, across, other, mate):
        pl.semaphore_signal(barrier, inc=1, device_id=to, device_id_type=MESH)
    pl.semaphore_wait(barrier, 7)
    for n in range(len(local)):
        when(local[n][2], lambda n=n: local_copy(n).wait())

    def x_own(cond_r, cond_l):
        send("xr", jnp.where(x < 3, own, a_own), a_own, right_x, cond_r)
        send("xl", jnp.where(x > 0, a_own, own), a_own, left_x, cond_l)

    def z_own(cond_r, cond_l):
        send("zr", jnp.where(z < 3, own, a_own), a_own, right_z, cond_r)
        send("zl", jnp.where(z > 0, a_own, own), a_own, left_z, cond_l)

    def relay(name, even, place, at, to_r, to_l):
        src = jnp.where(even, place(dn(at)), place(up(at)))
        send(name + "r", src, src, to_r, even)
        send(name + "l", src, src, to_l, jnp.logical_not(even))

    def over(name, u, cond=None):
        send("o" + name, u, u, other, cond)

    x_even, z_even = lax.rem(x, 2) == 0, lax.rem(z, 2) == 0
    sign = {0: z_even, 1: jnp.logical_not(z_even), 2: z_even, 3: jnp.logical_not(z_even)}

    def row_on(n, zz):
        u = B(x, zz, k)
        send(f"y{n}", u, R(zz, k), across, y == 0)
        send(f"r{n}", jnp.where(x < 3, u, R(zz, k)), u, right_x, x < 3)
        send(f"l{n}", jnp.where(x > 0, R(zz, k), u), u, left_x, x == 0)

    def before_on(n, zz):
        arrived(R(zz, k), y == 1)
        u = B(x, zz, k)
        send(f"r{n}", jnp.where(x < 3, u, R(zz, k)), u, right_x, x == 3)
        send(f"l{n}", jnp.where(x > 0, R(zz, k), u), u, left_x, x > 0)
        if n == 0:
            over("p0", R(z, 1), k == 1)
        else:
            over(f"p{n}", R(zz, k), zz > z)

    zs = {0: z, 1: up(z), 2: op(z), 3: dn(z)}
    xs = {0: x, 1: up(x), 2: op(x), 3: dn(x)}

    def row_here(n):
        zz = zs[n]
        arrived(B(x, zz, k))
        row_on(n, zz)
        over(f"b{n}", B(x, zz, k), zz < z)

    def col_here(n):
        u = A(z, xs[n], k)
        arrived(u)
        send(f"zr{n}", u, u, right_z)
        send(f"zl{n}", u, u, left_z)
        over(f"a0{n}", u)

    def a_here(nx, nz):
        u = A(zs[nz], xs[nx], k)
        arrived(u)
        over(f"a{nz}{nx}", u)

    def a_relay(nx):
        a_here(nx, 1)
        a_here(nx, 3)
        relay(f"az{nx}", sign[nx], lambda zz: A(zz, xs[nx], k), z, right_z, left_z)

    def b_here(nx, nz):
        u = B(xs[nx], zs[nz], k)
        arrived(u)
        over(f"b{nx}{nz}", u)

    def b_relay(nz):
        b_here(1, nz)
        b_here(3, nz)
        relay(f"bx{nz}", x_even, lambda xx: B(xx, zs[nz], k), x, right_x, left_x)

    def handed(g, slab):
        for dx, dz in slab:
            xx, zz = xs[dx], zs[dz]
            if g == 0:
                arrived(A(zz, xx, o))
            elif dx:
                arrived(B(xx, zz, o))
            elif dz:
                arrived(jnp.where(zz < z, B(x, zz, o), R(zz, o)))
            else:
                arrived(jnp.where(k == 0, R(z, o), B(x, z, o)))

    def first():
        send("y", own, a_own, across, y == 0)
        send("bzr", b_own, b_own, right_z)
        send("bzl", b_own, b_own, left_z)
        x_own(x < 3, x == 0)
        z_own(z < 3, z == 0)
        row_on(0, z)
        send("own0", own, A(z, x, 0), other, k == 0)
        send("own1", b_own, B(x, z, 0), other, k == 0)

    first()

    docs = doc_ref[...]
    first1 = jnp.sum((docs < 1).astype(F32), keepdims=True).astype(jnp.int32)
    first2 = jnp.sum((docs < 2).astype(F32), keepdims=True).astype(jnp.int32)
    lane = lax.broadcasted_iota(jnp.int32, (1, 128), 1)
    none = jnp.int32(1 << 30)
    lo = jnp.where(lane == 0, 0, jnp.where(lane == 1, first1, jnp.where(lane == 2, first2, jnp.where(lane == 3, -none, none))))
    hi = jnp.where(lane == 0, first1, jnp.where(lane == 1, first2, jnp.where(lane == 2, none, jnp.where(lane == 3, 0, -none))))
    p = x * 4 + z
    me = i * 256

    def mark(u, _):
        c, kk = u // 2, lax.rem(u, 2)
        yy = jnp.where(c < p, y, y - 1)
        base = ((yy * 16 + c) * 2 + kk) * 256
        inner = jnp.where(kk == k, -100000, jnp.where(k == 0, ((y * 16 - 16 + c) * 2 + 1) * 256, (y * 16 + c) * 512))
        base = jnp.where(u == 32, me, jnp.where(c == p, inner, base))
        row = base + lax.broadcasted_iota(jnp.int32, (256, 128), 0)
        aug[u] = jnp.where((row >= lo) & (row < hi), 1.0, 0.0).astype(BF16)
        return 0

    lax.fori_loop(0, 33, mark, 0)
    pos = me + lax.broadcasted_iota(jnp.int32, (128, 256), 1)
    mine = (pos >= first1).astype(jnp.int32) + (pos >= first2).astype(jnp.int32)
    d = lax.broadcasted_iota(jnp.int32, (128, 256), 0)
    qaug[...] = jnp.where((d < 4) & ((d == 3) | (mine != d)), FAR, 0.0).astype(BF16)

    def query(jt):
        top = jnp.concatenate([q_ref[2 * jt], q_ref[2 * jt + 1]], axis=1)
        low = jnp.concatenate([qaug[...], qaug[...]], axis=1)
        return jnp.concatenate([top, low], axis=0)

    def keys(u, au):
        return jnp.concatenate([buf[u, 0:256, :], aug[au]], axis=1)

    def values(u):
        return jnp.concatenate([buf[u, 256:384, :], buf[u, 384:512, :]], axis=1)

    def eighths(a, f):
        return f(a.reshape(a.shape[0] // 8, 8, T), axis=0)

    def own_block(g):
        u = own if g == 0 else b_own

        def tile(j, _):
            jt = g * 4 + j
            s = jnp.dot(keys(u, 32), query(jt), preferred_element_type=F32)
            key = lax.broadcasted_iota(jnp.int32, (256, T), 0)
            tok = lax.rem(lax.broadcasted_iota(jnp.int32, (256, T), 1), 256)
            s = jnp.where(key <= tok, s, FAR)
            m = jnp.max(s, axis=0, keepdims=True)
            w = jnp.exp2((s - m) * scale)
            mm[jt] = m
            ll[jt] = eighths(w, jnp.sum)
            acc[jt] = jnp.dot(values(u), w.astype(BF16), preferred_element_type=F32)
            return 0

        lax.fori_loop(0, 4, tile, 0)

    def chips(g, slab):
        found = []
        for dx, dz in slab:
            xx, zz = xs[dx], zs[dz]
            if g == 0:
                c = zz * 4 + xx
            elif dx:
                c = 16 + xx * 4 + zz
            elif dz:
                c = jnp.where(zz < z, 16 + x * 4 + zz, 32 + zz)
            else:
                c = jnp.where(k == 0, 32 + z, 16 + x * 4 + z)
            found.append((c * 2, (xx * 4 + zz) * 2))
        return found

    def step(cur, jt, m_cur, nxt, jn):
        if nxt is not None:
            q = query(jn)
        if cur is not None:
            m_old = mm[jt]
            m_new = jnp.maximum(m_old, m_cur)
            alpha = jnp.exp2((m_old - m_new) * scale)
            mm[jt] = m_new
            out = acc[jt] * alpha
            total = ll[jt] * alpha
        best = None
        for b in range(U // KB):
            rows = slice(b * KB, (b + 1) * KB)
            if cur is not None:
                w = jnp.exp2((s_ref[rows] - m_new) * scale)
                total = total + eighths(w, jnp.sum)
                w = w.astype(BF16)
            if nxt is not None:
                u, au = nxt[b // 2]
                s = jnp.dot(keys(u + b % 2, au + b % 2), q, preferred_element_type=F32)
                high = eighths(s, jnp.max)
                best = high if best is None else jnp.maximum(best, high)
                s_ref[rows] = s
            if cur is not None:
                out = out + jnp.dot(values(cur[b // 2][0] + b % 2), w, preferred_element_type=F32)
        if cur is not None:
            acc[jt] = out
            ll[jt] = total
        return None if nxt is None else jnp.max(best, axis=0, keepdims=True)

    def finish(jt):
        total = jnp.sum(ll[jt], axis=0, keepdims=True)
        done = acc[jt] / total
        for n in range(2):
            head = done[:, n * 256:(n + 1) * 256].T.astype(BF16)
            keep = jnp.where(h == 0, head[:128], head[128:])
            give = jnp.where(h == 0, head[128:], head[:128])
            obuf[h * 16 + 2 * jt + n] = keep
            sbuf[2 * jt + n] = give

    def give(jt):
        return pltpu.make_async_remote_copy(
            src_ref=sbuf.at[pl.ds(2 * jt, 2)], dst_ref=obuf.at[pl.ds(h * 16 + 2 * jt, 2)],
            send_sem=osend.at[jt], recv_sem=orecv.at[jt], device_id=mate, device_id_type=MESH)

    def put(jt, whose):
        at = pl.ds(whose * 16 + 2 * jt, 2)
        return pltpu.make_async_copy(obuf.at[at], out_ref.at[at], fsem.at[jt + 8 * (0 if whose is h else 1)])

    def e1():
        arrived(a_own, y == 1)
        x_own(x == 3, x > 0)
        z_own(z == 3, z > 0)
        over("a00", A(z, x, 1), k == 1)

    def f1():
        row_here(1)
        row_here(3)
        relay("bz", z_even, lambda zz: B(x, zz, k), z, right_z, left_z)

    def e2():
        col_here(1)
        col_here(3)
        relay("ax", x_even, lambda xx: A(z, xx, k), x, right_x, left_x)

    def e3():
        a_relay(0)

    e1()
    own_block(0)
    f1()
    before_on(0, z)
    e2()
    own_block(1)
    e3()
    handed(*SLABS[0])

    events = {
        0: [(0, [(row_here, 2)]),
            (1, [(col_here, 2), (before_on, 1, zs[1]), (before_on, 3, zs[3])]),
            (2, [(a_here, 0, 2), (b_relay, 0)])],
        1: [(0, [(a_relay, 1)]), (1, [(before_on, 2, zs[2])]), (2, [(a_relay, 3), (b_relay, 1)])],
        2: [(0, [(a_relay, 2)]), (1, [(b_relay, 3)]), (2, [(a_here, 1, 2), (a_here, 3, 2), (b_here, 2, 0)])],
        3: [(0, [(b_relay, 2)]), (1, [(a_here, 2, 2)]), (2, [(b_here, 2, 1)])],
        4: [(0, [(b_here, 2, 3)]), (3, [(b_here, 2, 2)])],
    }

    def happen(event):
        for f, *args in event:
            f(*args)

    places = [chips(*s) for s in SLABS]
    m = step(None, None, None, places[0], SLABS[0][0] * 4)
    for n, (g, _) in enumerate(SLABS):
        cur = places[n]
        last = n == len(SLABS) - 1
        ends = n == 4 or last

        def one(j, m, n=n, g=g, cur=cur, last=last, ends=ends):
            for at, event in events.get(n, ()):
                pl.when(j == at)(lambda event=event: happen(event))
            if not last:
                pl.when(j == 3)(lambda: handed(*SLABS[n + 1]))
            jt = g * 4 + j
            if last:
                nxt, jn = cur, jt + 1
            else:
                nxt = [(jnp.where(j < 3, a, c), jnp.where(j < 3, b, d)) for (a, b), (c, d) in zip(cur, places[n + 1])]
                jn = jnp.where(j < 3, jt + 1, SLABS[n + 1][0] * 4)
            m = step(cur, jt, m, nxt, jn)
            if ends:
                @pl.when(j > 0)
                def _():
                    give(jt - 1).start()
                    put(jt - 1, h).start()
                finish(jt)
            return m

        m = lax.fori_loop(0, 3 if last else 4, one, m)
        if n == 4:
            give(3).start()
            put(3, h).start()
    give(6).start()
    put(6, h).start()
    step(places[7], 7, m, None, None)
    finish(7)
    give(7).start()
    put(7, h).start()
    theirs = 1 - h
    for jt in range(8):
        give(jt).wait_recv()
        put(jt, theirs).start()
    ending[0] = True
    for f in (first, e1, f1, lambda: before_on(0, z), e2, e3):
        f()
    for n in events:
        for _, event in events[n]:
            happen(event)
    for jt in range(8):
        give(jt).wait_send()
        put(jt, h).wait()
        put(jt, theirs).wait()


N_SENDS = 128


def body(queries, key_rows, value_vectors, doc_ids):
    tokens, heads, size = queries.shape
    groups = key_rows.shape[1]
    q = queries.transpose(1, 2, 0)
    kk = key_rows.transpose(1, 0, 2)
    vv = value_vectors.reshape(2, 128, groups, size).transpose(2, 0, 3, 1).reshape(groups, 256, 128)
    kv = jnp.concatenate([kk, vv], axis=1)
    scale = LOG2E * size ** -0.5
    vmem, anyspace = pl.BlockSpec(memory_space=pltpu.VMEM), pl.BlockSpec(memory_space=pl.ANY)
    out = pl.pallas_call(
        functools.partial(kernel, scale),
        out_shape=jax.ShapeDtypeStruct((2 * heads, 128, size), BF16),
        in_specs=[vmem, anyspace, vmem],
        out_specs=anyspace,
        scratch_shapes=[
            pltpu.VMEM((UNITS, 512, 128), BF16),
            pltpu.VMEM((33, 256, 128), BF16),
            pltpu.VMEM((128, 256), BF16),
            pltpu.VMEM((U, T), F32),
            pltpu.VMEM((8, 128, T), F32),
            pltpu.VMEM((8, 1, T), F32),
            pltpu.VMEM((8, 8, T), F32),
            pltpu.VMEM((2 * heads, 128, size), BF16),
            pltpu.VMEM((heads, 128, size), BF16),
            pltpu.SemaphoreType.DMA((7,)),
            pltpu.SemaphoreType.DMA((N_SENDS,)),
            pltpu.SemaphoreType.DMA((UNITS,)),
            pltpu.SemaphoreType.DMA((8,)),
            pltpu.SemaphoreType.DMA((8,)),
            pltpu.SemaphoreType.DMA((16,)),
        ],
        compiler_params=pltpu.CompilerParams(
            collective_id=0, has_side_effects=True, vmem_limit_bytes=60 * 1024 * 1024),
    )(q, kv, doc_ids.reshape(128, 128))
    return out.transpose(1, 0, 2)


def solution(mesh):
    placed = (P("ctx", "head", None), P("ctx", "head", None), P("ctx", "head", None), P())
    return jax.shard_map(
        body, mesh=mesh, in_specs=placed, out_specs=P(("ctx", "head"), None, None), check_vma=False
    )
```

time: 420 us -> 78.9 us (0.19)
  the two profiles are of different devices: /device:TPU:8 before, /device:TPU:1 now
where the time goes in v1:
time: 78.9 us; the launch traced here: 78.7 us
  Pallas kernels  71.5 us (91%)
  local copies, waits for them, and re-layouts  6.48 us (8%)
    pallas_call x1, Pallas kernels, body(): pl.pallas_call(functools.partial(kernel, scale), out_shape=jax.ShapeDtype...  71.5 us
    transpose x1, local copies, waits for them, and re-layouts, body(): return out.transpose(1, 0, 2)  2.87 us
    unnamed x4, local copies, waits for them, and re-layouts  2.58 us

profile of v1, /device:TPU:1, one launch (start us, length us, event | category | flops | bytes accessed | tf_op | source)
XLA Modules:
  0.0 78.7 jit_solution(10207677360582928818)
XLA Ops:
  0.0 0.0 copy-start
  0.0 1.0 %copy.10 = bf16[256,2,128]{2,0,1:T(8,128)(2,1)S(1)} copy(bf16[256,2,128]{2,1,0:T(2,128)(2,1)} %param.5) | data formatting | bytes 262144 | tf_op args[1]
  1.0 1.0 %copy.7 = bf16[2,128,2,128]{1,3,0,2:T(8,128)(2,1)S(1)} copy(bf16[2,128,2,128]{3,2,1,0:T(2,128)(2,1)} %bitcast.14) | data formatting | bytes 262144 | tf_op jit(solution)/shard_map/reshape | solution.py:414
  2.1 0.7 pad_maximum_fusion.kv_ref
  2.8 0.0 copy-done
  2.8 1.6 %copy.5 = bf16[256,16,128]{0,2,1:T(8,128)(2,1)} copy(bf16[256,16,128]{2,1,0:T(8,128)(2,1)S(1)} %copy-done) | data formatting | bytes 2097152 | tf_op args[0]
  4.3 71.5 %shard_map.46 = bf16[32,128,128]{2,1,0:T(8,128)(2,1)} custom-call(bf16[16,128,256]{2,1,0:T(8,128)(2,1)} %bitcast.11, bf16[2,512,128]{2,1,0:T(8,128)(2,1)} %pad_maximum_fusion.kv_ref, s32[128,128]{1,0:T(8,128)} %bitcast.15), custom_call_target="tpu_custom_call" | custom-call | tf_op jit(solution)/shard_map/pallas_call | solution.py:418
  75.8 2.9 %copy.8 = bf16[128,32,128]{2,1,0:T(8,128)(2,1)} copy(bf16[128,32,128]{2,0,1:T(8,128)(2,1)} %bitcast.10) | data formatting | bytes 2097152 | tf_op jit(solution)/shard_map/transpose | solution.py:443
Async XLA Ops:
  0.0 2.8 %copy-start = (bf16[256,16,128]{2,1,0:T(8,128)(2,1)S(1)}, bf16[256,16,128]{2,1,0:T(8,128)(2,1)}, u32[]{:S(2)}) copy-start(bf16[256,16,128]{2,1,0:T(8,128)(2,1)} %param.4) | copy-start | bytes 3145732

commit v2 on v1

--- a/solution.py
+++ b/solution.py
@@ -20,11 +20,32 @@
 SECOND = ((0, 0), (2, 0), (0, 2), (1, 1))
 THIRD = ((1, 3), (3, 1), (3, 3), (2, 1))
 LAST = ((2, 3), (1, 2), (3, 2), (2, 2))
+TIMETABLE = {
+    1: ("e1", "f1", "f1b"),
+    2: ("p0",),
+    3: ("e2b", "a0", "a0b", "e2"),
+    5: ("row2",),
+    6: ("p1", "b0", "p3"),
+    7: ("b0b",),
+    8: ("col2",),
+    10: ("a1", "a3b", "a02", "a1b"),
+    11: ("b3",),
+    12: ("a2", "a3"),
+    13: ("p2",),
+    15: ("a12", "b1", "a2b"),
+    17: ("b1b",),
+    18: ("a32", "b2", "a22"),
+    20: ("b2b", "b3b"),
+    22: ("b23",),
+    23: ("b20",),
+    24: ("b21",),
+    27: ("b22",),
+}
 SLABS = ((0, NEAR), (1, NEAR), (0, SECOND), (0, THIRD), (0, LAST), (1, SECOND), (1, THIRD), (1, LAST))
 
 
-def kernel(scale, q_ref, kv_ref, doc_ref, out_ref, buf, aug, qaug, s_ref, acc, mm, ll, obuf, sbuf,
-           lsem, ssem, rsem, osend, orecv, fsem):
+def kernel(scale, q_hbm, k_hbm, v_hbm, doc_ref, out_ref, q_raw, q_rows, q_ref, buf, aug, qaug, s_ref, acc, mm, ll, obuf, sbuf,
+           lsem, qsem, ysem, ssem, rsem, osend, orecv, fsem):
     i = lax.axis_index("ctx")
     h = lax.axis_index("head")
     k = lax.rem(i, 2)
@@ -50,10 +71,11 @@
     sends = {}
     ending = [False]
 
-    def copy(n, src, dst, to):
+    def copy(n, src, dst, to, half=None, sem=None):
+        part = () if half is None else (pl.ds(256 * half, 256),)
         return pltpu.make_async_remote_copy(
-            src_ref=buf.at[src], dst_ref=buf.at[dst], send_sem=ssem.at[n], recv_sem=rsem.at[dst],
-            device_id=to, device_id_type=MESH)
+            src_ref=buf.at[(src,) + part], dst_ref=buf.at[(dst,) + part], send_sem=ssem.at[n],
+            recv_sem=rsem.at[dst] if sem is None else sem, device_id=to, device_id_type=MESH)
 
     def when(cond, f):
         if cond is None:
@@ -61,11 +83,11 @@
         else:
             pl.when(cond)(f)
 
-    def send(name, src, dst, to, cond=None):
+    def send(name, src, dst, to, cond=None, half=None, sem=None):
         n = sends.setdefault(name, len(sends))
 
         def go():
-            c = copy(n, src, dst, to)
+            c = copy(n, src, dst, to, half, sem)
             c.wait_send() if ending[0] else c.start()
 
         when(cond, go)
@@ -78,12 +100,25 @@
     a_own, b_own = A(z, x, k), B(x, z, k)
     local = [(0, own, None), (1, b_own, None), (0, a_own, y == 0)] + [(1, R(n, k), y == 0) for n in range(4)]
 
-    def local_copy(n):
-        g, u, _ = local[n]
-        return pltpu.make_async_copy(kv_ref.at[g], buf.at[u], lsem.at[n])
+    class local_copy:
+        def __init__(self, n):
+            g, u, _ = local[n]
+            self.both = [
+                pltpu.make_async_copy(k_hbm.at[g], buf.at[u, 0:256], lsem.at[2 * n]),
+                pltpu.make_async_copy(v_hbm.at[g], buf.at[u, 256:512], lsem.at[2 * n + 1])]
+
+        def start(self):
+            for c in self.both:
+                c.start()
+
+        def wait(self):
+            for c in self.both:
+                c.wait()
 
     for n in range(len(local)):
         when(local[n][2], lambda n=n: local_copy(n).start())
+    load_q = pltpu.make_async_copy(q_hbm, q_raw, qsem)
+    load_q.start()
     barrier = pltpu.get_barrier_semaphore()
     for to in (right_x, left_x, right_z, left_z, across, other, mate):
         pl.semaphore_signal(barrier, inc=1, device_id=to, device_id_type=MESH)
@@ -91,14 +126,6 @@
     for n in range(len(local)):
         when(local[n][2], lambda n=n: local_copy(n).wait())
 
-    def x_own(cond_r, cond_l):
-        send("xr", jnp.where(x < 3, own, a_own), a_own, right_x, cond_r)
-        send("xl", jnp.where(x > 0, a_own, own), a_own, left_x, cond_l)
-
-    def z_own(cond_r, cond_l):
-        send("zr", jnp.where(z < 3, own, a_own), a_own, right_z, cond_r)
-        send("zl", jnp.where(z > 0, a_own, own), a_own, left_z, cond_l)
-
     def relay(name, even, place, at, to_r, to_l):
         src = jnp.where(even, place(dn(at)), place(up(at)))
         send(name + "r", src, src, to_r, even)
@@ -110,17 +137,17 @@
     x_even, z_even = lax.rem(x, 2) == 0, lax.rem(z, 2) == 0
     sign = {0: z_even, 1: jnp.logical_not(z_even), 2: z_even, 3: jnp.logical_not(z_even)}
 
-    def row_on(n, zz):
+    def row_on(name, zz):
         u = B(x, zz, k)
-        send(f"y{n}", u, R(zz, k), across, y == 0)
-        send(f"r{n}", jnp.where(x < 3, u, R(zz, k)), u, right_x, x < 3)
-        send(f"l{n}", jnp.where(x > 0, R(zz, k), u), u, left_x, x == 0)
+        send(name + "y", u, R(zz, k), across, y == 0)
+        send(name + "r", u, u, right_x, x < 3)
+        send(name + "l", u, u, left_x, x == 0)
 
     def before_on(n, zz):
         arrived(R(zz, k), y == 1)
         u = B(x, zz, k)
-        send(f"r{n}", jnp.where(x < 3, u, R(zz, k)), u, right_x, x == 3)
-        send(f"l{n}", jnp.where(x > 0, R(zz, k), u), u, left_x, x > 0)
+        send(f"pr{n}", R(zz, k), u, right_x, x == 3)
+        send(f"pl{n}", R(zz, k), u, left_x, x > 0)
         if n == 0:
             over("p0", R(z, 1), k == 1)
         else:
@@ -129,38 +156,76 @@
     zs = {0: z, 1: up(z), 2: op(z), 3: dn(z)}
     xs = {0: x, 1: up(x), 2: op(x), 3: dn(x)}
 
-    def row_here(n):
-        zz = zs[n]
+    def nearer(even, at, first):
+        return jnp.where(even == first, dn(at), up(at))
+
+    def row_here(name, zz, first=False):
         arrived(B(x, zz, k))
-        row_on(n, zz)
-        over(f"b{n}", B(x, zz, k), zz < z)
-
-    def col_here(n):
-        u = A(z, xs[n], k)
+        if first:
+            relay("bz", z_even, lambda c: B(x, c, k), z, right_z, left_z)
+        row_on(name, zz)
+        over(name, B(x, zz, k), zz < z)
+
+    def col_here(name, xx, first=False):
+        u = A(z, xx, k)
         arrived(u)
-        send(f"zr{n}", u, u, right_z)
-        send(f"zl{n}", u, u, left_z)
-        over(f"a0{n}", u)
-
-    def a_here(nx, nz):
-        u = A(zs[nz], xs[nx], k)
+        if first:
+            relay("ax", x_even, lambda c: A(z, c, k), x, right_x, left_x)
+        send(name + "zr", u, u, right_z)
+        send(name + "zl", u, u, left_z)
+        over(name, u)
+
+    def a_here(n, zz, first=False):
+        u = A(zz, xs[n], k)
         arrived(u)
-        over(f"a{nz}{nx}", u)
-
-    def a_relay(nx):
-        a_here(nx, 1)
-        a_here(nx, 3)
-        relay(f"az{nx}", sign[nx], lambda zz: A(zz, xs[nx], k), z, right_z, left_z)
-
-    def b_here(nx, nz):
-        u = B(xs[nx], zs[nz], k)
+        if first:
+            relay(f"az{n}", sign[n], lambda c: A(c, xs[n], k), z, right_z, left_z)
+        over(f"a{n}{'n' if first else 'f'}", u)
+
+    def a_opposite(n):
+        u = A(zs[2], xs[n], k)
         arrived(u)
-        over(f"b{nx}{nz}", u)
-
-    def b_relay(nz):
-        b_here(1, nz)
-        b_here(3, nz)
-        relay(f"bx{nz}", x_even, lambda xx: B(xx, zs[nz], k), x, right_x, left_x)
+        over(f"a{n}2", u)
+
+    def b_here(n, xx, first=False):
+        u = B(xx, zs[n], k)
+        arrived(u)
+        if first:
+            relay(f"bx{n}", x_even, lambda c: B(c, zs[n], k), x, right_x, left_x)
+        over(f"b{n}{'n' if first else 'f'}", u)
+
+    def b_opposite(n):
+        u = B(xs[2], zs[n], k)
+        arrived(u)
+        over(f"b2{n}", u)
+
+    def previous():
+        for half in range(2):
+            if not ending[0]:
+                when(y == 1, lambda: copy(0, a_own, a_own, other, half, ysem.at[half]).wait_recv())
+            send(f"pxr{half}", a_own, a_own, right_x, x == 3, half)
+            send(f"pxl{half}", a_own, a_own, left_x, x > 0, half)
+            send(f"pzr{half}", a_own, a_own, right_z, z == 3, half)
+            send(f"pzl{half}", a_own, a_own, left_z, z > 0, half)
+        over("a00", A(z, x, 1), k == 1)
+
+    happenings = {
+        "e1": previous,
+        "f1": lambda: row_here("f1", nearer(z_even, z, True), True),
+        "f1b": lambda: row_here("f1b", nearer(z_even, z, False)),
+        "row2": lambda: row_here("row2", zs[2]),
+        "e2": lambda: col_here("e2", nearer(x_even, x, True), True),
+        "e2b": lambda: col_here("e2b", nearer(x_even, x, False)),
+        "col2": lambda: col_here("col2", xs[2]),
+    }
+    for n in range(4):
+        happenings[f"p{n}"] = lambda n=n: before_on(n, zs[n])
+        happenings[f"a{n}"] = lambda n=n: a_here(n, nearer(sign[n], z, True), True)
+        happenings[f"a{n}b"] = lambda n=n: a_here(n, nearer(sign[n], z, False))
+        happenings[f"a{n}2"] = lambda n=n: a_opposite(n)
+        happenings[f"b{n}"] = lambda n=n: b_here(n, nearer(x_even, x, True), True)
+        happenings[f"b{n}b"] = lambda n=n: b_here(n, nearer(x_even, x, False))
+        happenings[f"b2{n}"] = lambda n=n: b_opposite(n)
 
     def handed(g, slab):
         for dx, dz in slab:
@@ -175,12 +240,15 @@
                 arrived(jnp.where(k == 0, R(z, o), B(x, z, o)))
 
     def first():
-        send("y", own, a_own, across, y == 0)
+        send("y0", own, a_own, across, y == 0, 0, ysem.at[0])
+        send("y1", own, a_own, across, y == 0, 1, ysem.at[1])
         send("bzr", b_own, b_own, right_z)
         send("bzl", b_own, b_own, left_z)
-        x_own(x < 3, x == 0)
-        z_own(z < 3, z == 0)
-        row_on(0, z)
+        send("xr", own, a_own, right_x, x < 3)
+        send("xl", own, a_own, left_x, x == 0)
+        send("zr", own, a_own, right_z, z < 3)
+        send("zl", own, a_own, left_z, z == 0)
+        row_on("own", z)
         send("own0", own, A(z, x, 0), other, k == 0)
         send("own1", b_own, B(x, z, 0), other, k == 0)
 
@@ -206,7 +274,6 @@
         aug[u] = jnp.where((row >= lo) & (row < hi), 1.0, 0.0).astype(BF16)
         return 0
 
-    lax.fori_loop(0, 33, mark, 0)
     pos = me + lax.broadcasted_iota(jnp.int32, (128, 256), 1)
     mine = (pos >= first1).astype(jnp.int32) + (pos >= first2).astype(jnp.int32)
     d = lax.broadcasted_iota(jnp.int32, (128, 256), 0)
@@ -308,95 +375,90 @@
         at = pl.ds(whose * 16 + 2 * jt, 2)
         return pltpu.make_async_copy(obuf.at[at], out_ref.at[at], fsem.at[jt + 8 * (0 if whose is h else 1)])
 
-    def e1():
-        arrived(a_own, y == 1)
-        x_own(x == 3, x > 0)
-        z_own(z == 3, z > 0)
-        over("a00", A(z, x, 1), k == 1)
-
-    def f1():
-        row_here(1)
-        row_here(3)
-        relay("bz", z_even, lambda zz: B(x, zz, k), z, right_z, left_z)
-
-    def e2():
-        col_here(1)
-        col_here(3)
-        relay("ax", x_even, lambda xx: A(z, xx, k), x, right_x, left_x)
-
-    def e3():
-        a_relay(0)
-
-    e1()
+    def happen(p):
+        for name in TIMETABLE.get(p, ()):
+            happenings[name]()
+
+    happen(0)
+    lax.fori_loop(0, 33, mark, 0)
+    load_q.wait()
+    r = lax.broadcasted_iota(jnp.int32, (256, 256), 0)
+    c = lax.broadcasted_iota(jnp.int32, (256, 256), 1)
+    order = jnp.where(c == lax.rem(r, 16) * 16 + r // 16, 1.0, 0.0).astype(BF16)
+
+    def by_head(n, _):
+        rows = q_raw[pl.ds(pl.multiple_of(n * 256, 256), 256), :]
+        rows = jnp.dot(order, rows, preferred_element_type=F32).astype(BF16)
+        for head in range(16):
+            q_rows[head, pl.ds(pl.multiple_of(n * 16, 16), 16), :] = rows[head * 16:(head + 1) * 16]
+        return 0
+
+    def turn(n, _):
+        q_ref[2 * n] = q_rows[2 * n].T
+        q_ref[2 * n + 1] = q_rows[2 * n + 1].T
+        return 0
+
+    lax.fori_loop(0, 16, by_head, 0, unroll=8)
+    lax.fori_loop(0, 8, turn, 0, unroll=4)
+    happen(1)
     own_block(0)
-    f1()
-    before_on(0, z)
-    e2()
+    happen(2)
     own_block(1)
-    e3()
+    happen(3)
     handed(*SLABS[0])
-
-    events = {
-        0: [(0, [(row_here, 2)]),
-            (1, [(col_here, 2), (before_on, 1, zs[1]), (before_on, 3, zs[3])]),
-            (2, [(a_here, 0, 2), (b_relay, 0)])],
-        1: [(0, [(a_relay, 1)]), (1, [(before_on, 2, zs[2])]), (2, [(a_relay, 3), (b_relay, 1)])],
-        2: [(0, [(a_relay, 2)]), (1, [(b_relay, 3)]), (2, [(a_here, 1, 2), (a_here, 3, 2), (b_here, 2, 0)])],
-        3: [(0, [(b_relay, 2)]), (1, [(a_here, 2, 2)]), (2, [(b_here, 2, 1)])],
-        4: [(0, [(b_here, 2, 3)]), (3, [(b_here, 2, 2)])],
-    }
-
-    def happen(event):
-        for f, *args in event:
-            f(*args)
-
     places = [chips(*s) for s in SLABS]
+
+    def out_of(jt):
+        give(jt).start()
+        put(jt, h).start()
+
     m = step(None, None, None, places[0], SLABS[0][0] * 4)
-    for n, (g, _) in enumerate(SLABS):
-        cur = places[n]
-        last = n == len(SLABS) - 1
-        ends = n == 4 or last
-
-        def one(j, m, n=n, g=g, cur=cur, last=last, ends=ends):
-            for at, event in events.get(n, ()):
-                pl.when(j == at)(lambda event=event: happen(event))
-            if not last:
-                pl.when(j == 3)(lambda: handed(*SLABS[n + 1]))
+    for n in range(6):
+        g, cur = SLABS[n][0], places[n]
+
+        def one(j, m, n=n, g=g, cur=cur):
+            for at in range(4):
+                if 4 + 4 * n + at in TIMETABLE:
+                    pl.when(j == at)(lambda at=at: happen(4 + 4 * n + at))
+            pl.when(j == 3)(lambda: handed(*SLABS[n + 1]))
             jt = g * 4 + j
-            if last:
-                nxt, jn = cur, jt + 1
-            else:
-                nxt = [(jnp.where(j < 3, a, c), jnp.where(j < 3, b, d)) for (a, b), (c, d) in zip(cur, places[n + 1])]
-                jn = jnp.where(j < 3, jt + 1, SLABS[n + 1][0] * 4)
-            m = step(cur, jt, m, nxt, jn)
-            if ends:
-                @pl.when(j > 0)
-                def _():
-                    give(jt - 1).start()
-                    put(jt - 1, h).start()
+            nxt = [(jnp.where(j < 3, a, c), jnp.where(j < 3, b, d)) for (a, b), (c, d) in zip(cur, places[n + 1])]
+            m = step(cur, jt, m, nxt, jnp.where(j < 3, jt + 1, SLABS[n + 1][0] * 4))
+            if n == 4:
+                pl.when(j > 0)(lambda: out_of(jt - 1))
                 finish(jt)
             return m
 
-        m = lax.fori_loop(0, 3 if last else 4, one, m)
+        m = lax.fori_loop(0, 4, one, m)
         if n == 4:
-            give(3).start()
-            put(3, h).start()
-    give(6).start()
-    put(6, h).start()
+            out_of(3)
+
+    def two(j, m):
+        @pl.when(j == 0)
+        def _():
+            happen(28)
+            handed(*SLABS[7])
+        jt = 4 + j
+        m = step(places[6], jt, m, places[7], jt)
+        pl.when(j > 0)(lambda: out_of(jt - 1))
+        m = step(places[7], jt, m, places[6], jt + 1)
+        finish(jt)
+        return m
+
+    m = lax.fori_loop(0, 3, two, m)
+    m = step(places[6], 7, m, places[7], 7)
+    out_of(6)
     step(places[7], 7, m, None, None)
     finish(7)
-    give(7).start()
-    put(7, h).start()
+    out_of(7)
     theirs = 1 - h
     for jt in range(8):
         give(jt).wait_recv()
         put(jt, theirs).start()
     ending[0] = True
-    for f in (first, e1, f1, lambda: before_on(0, z), e2, e3):
-        f()
-    for n in events:
-        for _, event in events[n]:
-            happen(event)
+    first()
+    for p in TIMETABLE:
+        happen(p)
     for jt in range(8):
         give(jt).wait_send()
         put(jt, h).wait()
@@ -409,18 +471,20 @@
 def body(queries, key_rows, value_vectors, doc_ids):
     tokens, heads, size = queries.shape
     groups = key_rows.shape[1]
-    q = queries.transpose(1, 2, 0)
+    q = queries.reshape(tokens * heads, size)
     kk = key_rows.transpose(1, 0, 2)
     vv = value_vectors.reshape(2, 128, groups, size).transpose(2, 0, 3, 1).reshape(groups, 256, 128)
-    kv = jnp.concatenate([kk, vv], axis=1)
     scale = LOG2E * size ** -0.5
     vmem, anyspace = pl.BlockSpec(memory_space=pltpu.VMEM), pl.BlockSpec(memory_space=pl.ANY)
     out = pl.pallas_call(
         functools.partial(kernel, scale),
         out_shape=jax.ShapeDtypeStruct((2 * heads, 128, size), BF16),
-        in_specs=[vmem, anyspace, vmem],
+        in_specs=[anyspace, anyspace, anyspace, vmem],
         out_specs=anyspace,
         scratch_shapes=[
+            pltpu.VMEM((tokens * heads, size), BF16),
+            pltpu.VMEM((heads, tokens, size), BF16),
+            pltpu.VMEM((heads, size, tokens), BF16),
             pltpu.VMEM((UNITS, 512, 128), BF16),
             pltpu.VMEM((33, 256, 128), BF16),
             pltpu.VMEM((128, 256), BF16),
@@ -430,7 +494,9 @@
             pltpu.VMEM((8, 8, T), F32),
             pltpu.VMEM((2 * heads, 128, size), BF16),
             pltpu.VMEM((heads, 128, size), BF16),
-            pltpu.SemaphoreType.DMA((7,)),
+            pltpu.SemaphoreType.DMA((14,)),
+            pltpu.SemaphoreType.DMA,
+            pltpu.SemaphoreType.DMA((2,)),
             pltpu.SemaphoreType.DMA((N_SENDS,)),
             pltpu.SemaphoreType.DMA((UNITS,)),
             pltpu.SemaphoreType.DMA((8,)),
@@ -439,7 +505,7 @@
         ],
         compiler_params=pltpu.CompilerParams(
             collective_id=0, has_side_effects=True, vmem_limit_bytes=60 * 1024 * 1024),
-    )(q, kv, doc_ids.reshape(128, 128))
+    )(q, kk, vv, doc_ids.reshape(128, 128))
     return out.transpose(1, 0, 2)
 
 

time: 78.9 us -> 72.9 us (0.924)
  Pallas kernels: 71.5 us -> 67.4 us
  local copies, waits for them, and re-layouts: 6.48 us -> 5.25 us
    pallas_call x1, Pallas kernels: 71.5 us -> 67.4 us  [body(): pl.pallas_call(functools.partial(kernel, scale), out_shape=jax.ShapeDtype...]
    unnamed x4 -> x3, local copies, waits for them, and re-layouts: 2.58 us -> 1.62 us
where the time goes in v2:
time: 72.9 us; the launch traced here: 72.7 us
  Pallas kernels  67.4 us (92%)
  local copies, waits for them, and re-layouts  5.25 us (7%)
    pallas_call x1, Pallas kernels, body(): pl.pallas_call(functools.partial(kernel, scale), out_shape=jax.ShapeDtype...  67.4 us
    transpose x1, local copies, waits for them, and re-layouts, body(): return out.transpose(1, 0, 2)  2.87 us
    unnamed x3, local copies, waits for them, and re-layouts  1.62 us

profile of v2, /device:TPU:1, one launch (start us, length us, event | category | flops | bytes accessed | tf_op | source)
XLA Modules:
  0.0 72.7 jit_solution(9431052088809726591)
XLA Ops:
  0.0 0.0 copy-start
  0.0 1.6 %copy.9 = bf16[256,2,128]{2,0,1:T(8,128)(2,1)} copy(bf16[256,2,128]{2,1,0:T(2,128)(2,1)} %param.5) | data formatting | bytes 262144 | tf_op args[1]
  1.6 0.0 copy-done
  1.6 0.8 %copy.6 = bf16[2,128,2,128]{1,3,0,2:T(8,128)(2,1)} copy(bf16[2,128,2,128]{3,2,1,0:T(2,128)(2,1)S(1)} %bitcast.14) | data formatting | bytes 262144 | tf_op jit(solution)/shard_map/reshape | solution.py:476
  2.4 67.4 %shard_map.46 = bf16[32,128,128]{2,1,0:T(8,128)(2,1)} custom-call(bf16[4096,128]{1,0:T(8,128)(2,1)} %bitcast.11, bf16[2,256,128]{2,1,0:T(8,128)(2,1)} %bitcast.12, bf16[2,256,128]{2,1,0:T(8,128)(2,1)} %bitcast.13, s32[128,128]{1,0:T(8,128)} %bitcast.15), custom_call_target="tpu_custom_call" | custom-call | tf_op jit(solution)/shard_map/pallas_call | solution.py:479
  69.8 2.9 %copy.7 = bf16[128,32,128]{2,1,0:T(8,128)(2,1)} copy(bf16[128,32,128]{2,0,1:T(8,128)(2,1)} %bitcast.10) | data formatting | bytes 2097152 | tf_op jit(solution)/shard_map/transpose | solution.py:509
Async XLA Ops:
  0.0 1.6 %copy-start = (bf16[256,2,128]{2,1,0:T(2,128)(2,1)S(1)}, bf16[256,2,128]{2,1,0:T(2,128)(2,1)}, u32[]{:S(2)}) copy-start(bf16[256,2,128]{2,1,0:T(2,128)(2,1)} %param.6) | copy-start | bytes 393220

commit v3 on v2

--- a/solution.py
+++ b/solution.py
@@ -24,22 +24,21 @@
     1: ("e1", "f1", "f1b"),
     2: ("p0",),
     3: ("e2b", "a0", "a0b", "e2"),
-    5: ("row2",),
-    6: ("p1", "b0", "p3"),
-    7: ("b0b",),
-    8: ("col2",),
-    10: ("a1", "a3b", "a02", "a1b"),
-    11: ("b3",),
-    12: ("a2", "a3"),
-    13: ("p2",),
-    15: ("a12", "b1", "a2b"),
-    17: ("b1b",),
-    18: ("a32", "b2", "a22"),
-    20: ("b2b", "b3b"),
-    22: ("b23",),
-    23: ("b20",),
-    24: ("b21",),
-    27: ("b22",),
+    4: ("row2", "p1", "b0", "p3"),
+    5: ("b0b",),
+    6: ("col2",),
+    8: ("a1", "a3b", "a02", "a1b"),
+    9: ("b3",),
+    10: ("a2", "a3"),
+    11: ("p2",),
+    13: ("a12", "b1", "a2b"),
+    15: ("b1b",),
+    16: ("a32", "b2", "a22"),
+    18: ("b2b", "b3b"),
+    20: ("b23",),
+    21: ("b20",),
+    22: ("b21",),
+    25: ("b22",),
 }
 SLABS = ((0, NEAR), (1, NEAR), (0, SECOND), (0, THIRD), (0, LAST), (1, SECOND), (1, THIRD), (1, LAST))
 
@@ -363,17 +362,17 @@
             head = done[:, n * 256:(n + 1) * 256].T.astype(BF16)
             keep = jnp.where(h == 0, head[:128], head[128:])
             give = jnp.where(h == 0, head[128:], head[:128])
-            obuf[h * 16 + 2 * jt + n] = keep
+            obuf[2 * jt + n] = keep
             sbuf[2 * jt + n] = give
 
     def give(jt):
         return pltpu.make_async_remote_copy(
-            src_ref=sbuf.at[pl.ds(2 * jt, 2)], dst_ref=obuf.at[pl.ds(h * 16 + 2 * jt, 2)],
+            src_ref=sbuf.at[pl.ds(2 * jt, 2)], dst_ref=out_ref.at[pl.ds(h * 16 + 2 * jt, 2)],
             send_sem=osend.at[jt], recv_sem=orecv.at[jt], device_id=mate, device_id_type=MESH)
 
-    def put(jt, whose):
-        at = pl.ds(whose * 16 + 2 * jt, 2)
-        return pltpu.make_async_copy(obuf.at[at], out_ref.at[at], fsem.at[jt + 8 * (0 if whose is h else 1)])
+    def put(jt):
+        return pltpu.make_async_copy(
+            obuf.at[pl.ds(2 * jt, 2)], out_ref.at[pl.ds(h * 16 + 2 * jt, 2)], fsem.at[jt])
 
     def happen(p):
         for name in TIMETABLE.get(p, ()):
@@ -410,7 +409,7 @@
 
     def out_of(jt):
         give(jt).start()
-        put(jt, h).start()
+        put(jt).start()
 
     m = step(None, None, None, places[0], SLABS[0][0] * 4)
     for n in range(6):
@@ -451,18 +450,15 @@
     step(places[7], 7, m, None, None)
     finish(7)
     out_of(7)
-    theirs = 1 - h
-    for jt in range(8):
-        give(jt).wait_recv()
-        put(jt, theirs).start()
     ending[0] = True
     first()
     for p in TIMETABLE:
         happen(p)
     for jt in range(8):
         give(jt).wait_send()
-        put(jt, h).wait()
-        put(jt, theirs).wait()
+        put(jt).wait()
+    for jt in range(8):
+        give(jt).wait_recv()
 
 
 N_SENDS = 128
@@ -492,7 +488,7 @@
             pltpu.VMEM((8, 128, T), F32),
             pltpu.VMEM((8, 1, T), F32),
             pltpu.VMEM((8, 8, T), F32),
-            pltpu.VMEM((2 * heads, 128, size), BF16),
+            pltpu.VMEM((heads, 128, size), BF16),
             pltpu.VMEM((heads, 128, size), BF16),
             pltpu.SemaphoreType.DMA((14,)),
             pltpu.SemaphoreType.DMA,
@@ -501,7 +497,7 @@
             pltpu.SemaphoreType.DMA((UNITS,)),
             pltpu.SemaphoreType.DMA((8,)),
             pltpu.SemaphoreType.DMA((8,)),
-            pltpu.SemaphoreType.DMA((16,)),
+            pltpu.SemaphoreType.DMA((8,)),
         ],
         compiler_params=pltpu.CompilerParams(
             collective_id=0, has_side_effects=True, vmem_limit_bytes=60 * 1024 * 1024),

time: 72.9 us -> 69.7 us (0.956); the launches traced: 72.7 us -> 68.4 us
  Pallas kernels: 67.4 us -> 63.2 us
    pallas_call x1, Pallas kernels: 67.4 us -> 63.2 us  [body(): pl.pallas_call(functools.partial(kernel, scale), out_shape=jax.ShapeDtype...]
where the time goes in v3:
time: 69.7 us; the launch traced here: 68.4 us
  Pallas kernels  63.2 us (91%)
  local copies, waits for them, and re-layouts  5.25 us (8%)
    pallas_call x1, Pallas kernels, body(): pl.pallas_call(functools.partial(kernel, scale), out_shape=jax.ShapeDtype...  63.2 us
    transpose x1, local copies, waits for them, and re-layouts, body(): return out.transpose(1, 0, 2)  2.87 us
    unnamed x3, local copies, waits for them, and re-layouts  1.62 us

profile of v3, /device:TPU:1, one launch (start us, length us, event | category | flops | bytes accessed | tf_op | source)
XLA Modules:
  0.0 68.4 jit_solution(13534780104177088786)
XLA Ops:
  0.0 0.0 copy-start
  0.0 1.6 %copy.9 = bf16[256,2,128]{2,0,1:T(8,128)(2,1)} copy(bf16[256,2,128]{2,1,0:T(2,128)(2,1)} %param.5) | data formatting | bytes 262144 | tf_op args[1]
  1.6 0.0 copy-done
  1.6 0.8 %copy.6 = bf16[2,128,2,128]{1,3,0,2:T(8,128)(2,1)} copy(bf16[2,128,2,128]{3,2,1,0:T(2,128)(2,1)S(1)} %bitcast.14) | data formatting | bytes 262144 | tf_op jit(solution)/shard_map/reshape | solution.py:472
  2.4 63.2 %shard_map.46 = bf16[32,128,128]{2,1,0:T(8,128)(2,1)} custom-call(bf16[4096,128]{1,0:T(8,128)(2,1)} %bitcast.11, bf16[2,256,128]{2,1,0:T(8,128)(2,1)} %bitcast.12, bf16[2,256,128]{2,1,0:T(8,128)(2,1)} %bitcast.13, s32[128,128]{1,0:T(8,128)} %bitcast.15), custom_call_target="tpu_custom_call" | custom-call | tf_op jit(solution)/shard_map/pallas_call | solution.py:475
  65.6 2.9 %copy.7 = bf16[128,32,128]{2,1,0:T(8,128)(2,1)} copy(bf16[128,32,128]{2,0,1:T(8,128)(2,1)} %bitcast.10) | data formatting | bytes 2097152 | tf_op jit(solution)/shard_map/transpose | solution.py:505
Async XLA Ops:
  0.0 1.6 %copy-start = (bf16[256,2,128]{2,1,0:T(2,128)(2,1)S(1)}, bf16[256,2,128]{2,1,0:T(2,128)(2,1)}, u32[]{:S(2)}) copy-start(bf16[256,2,128]{2,1,0:T(2,128)(2,1)} %param.6) | copy-start | bytes 393220

commit v4 on v3

--- a/solution.py
+++ b/solution.py
@@ -23,7 +23,7 @@
 TIMETABLE = {
     1: ("e1", "f1", "f1b"),
     2: ("p0",),
-    3: ("e2b", "a0", "a0b", "e2"),
+    3: ("e2", "e2b", "a0", "a0b"),
     4: ("row2", "p1", "b0", "p3"),
     5: ("b0b",),
     6: ("col2",),
@@ -308,7 +308,7 @@
             acc[jt] = jnp.dot(values(u), w.astype(BF16), preferred_element_type=F32)
             return 0
 
-        lax.fori_loop(0, 4, tile, 0)
+        lax.fori_loop(0, 4, tile, 0, unroll=2)
 
     def chips(g, slab):
         found = []
@@ -379,7 +379,7 @@
             happenings[name]()
 
     happen(0)
-    lax.fori_loop(0, 33, mark, 0)
+    lax.fori_loop(0, 33, mark, 0, unroll=3)
     load_q.wait()
     r = lax.broadcasted_iota(jnp.int32, (256, 256), 0)
     c = lax.broadcasted_iota(jnp.int32, (256, 256), 1)

time: 69.7 us -> 69.7 us (level)
  no operation moved by 1% of the time
where the time goes in v4:
time: 69.7 us; the launch traced here: 68.7 us
  Pallas kernels  63.4 us (91%)
  local copies, waits for them, and re-layouts  5.25 us (8%)
    pallas_call x1, Pallas kernels, body(): pl.pallas_call(functools.partial(kernel, scale), out_shape=jax.ShapeDtype...  63.4 us
    transpose x1, local copies, waits for them, and re-layouts, body(): return out.transpose(1, 0, 2)  2.87 us
    unnamed x3, local copies, waits for them, and re-layouts  1.62 us

profile of v4, /device:TPU:1, one launch (start us, length us, event | category | flops | bytes accessed | tf_op | source)
XLA Modules:
  0.0 68.7 jit_solution(11300025700645659961)
XLA Ops:
  0.0 0.0 copy-start
  0.0 1.6 %copy.9 = bf16[256,2,128]{2,0,1:T(8,128)(2,1)} copy(bf16[256,2,128]{2,1,0:T(2,128)(2,1)} %param.5) | data formatting | bytes 262144 | tf_op args[1]
  1.6 0.0 copy-done
  1.6 0.8 %copy.6 = bf16[2,128,2,128]{1,3,0,2:T(8,128)(2,1)} copy(bf16[2,128,2,128]{3,2,1,0:T(2,128)(2,1)S(1)} %bitcast.14) | data formatting | bytes 262144 | tf_op jit(solution)/shard_map/reshape | solution.py:472
  2.4 63.4 %shard_map.46 = bf16[32,128,128]{2,1,0:T(8,128)(2,1)} custom-call(bf16[4096,128]{1,0:T(8,128)(2,1)} %bitcast.11, bf16[2,256,128]{2,1,0:T(8,128)(2,1)} %bitcast.12, bf16[2,256,128]{2,1,0:T(8,128)(2,1)} %bitcast.13, s32[128,128]{1,0:T(8,128)} %bitcast.15), custom_call_target="tpu_custom_call" | custom-call | tf_op jit(solution)/shard_map/pallas_call | solution.py:475
  65.8 2.9 %copy.7 = bf16[128,32,128]{2,1,0:T(8,128)(2,1)} copy(bf16[128,32,128]{2,0,1:T(8,128)(2,1)} %bitcast.10) | data formatting | bytes 2097152 | tf_op jit(solution)/shard_map/transpose | solution.py:505
Async XLA Ops:
  0.0 1.6 %copy-start = (bf16[256,2,128]{2,1,0:T(2,128)(2,1)S(1)}, bf16[256,2,128]{2,1,0:T(2,128)(2,1)}, u32[]{:S(2)}) copy-start(bf16[256,2,128]{2,1,0:T(2,128)(2,1)} %param.6) | copy-start | bytes 393220
